TPU v7x, 256 devices: a 8x8x2 block of a 8x8x16 slice. The times are simulated.
256 devices in a mesh: img: 2 (over z), ga: 16 (over y, core), band: 8 (over x).
Axes of the slice: x: 8, y: 8, z: 2, core: 2. Of those that a mesh axis runs over, the one named last changes fastest.
The devices are a block of a 8x8x16 slice.
Arguments:
- orbitals: bfloat16 [1536, 49152], P(('img', 'band'), 'ga'), parts along dimension 0, as said below
- kernel: float32 [49152], P('ga'), may hold values from 0.3 to 3
- block_vectors: bfloat16 [512, 49152], P(('img', 'band'), 'ga'), parts along dimension 0
Outputs:
- ace_vectors: bfloat16 [1536, 49152], P(('img', 'band'), 'ga'), parts along dimension 0
- exchange_block: bfloat16 [512, 49152], P(('img', 'band'), 'ga'), parts along dimension 0
There are 2 independent parts, one for each index of `img`. A program takes and returns all parts, laid end to end along the dimension named above; an argument that names none is the same for every part. Nothing has to cross between parts.
Inputs may be any that keep to these rules, and one draw needn't show every extreme that they name: `orbitals`: the bands of one image are linearly independent, and the block lies largely in their span.
All inputs are finite; a program needn't handle non-finite values.
Results may differ from a plain program's by a relative error of at most 0.02.
Values may be sent and summed in bfloat16 or wider, within the bound.
A program may use at most 64 MiB of HBM per device.

v0:
```python
import jax
import jax.numpy as jnp
from jax import lax
from jax.sharding import PartitionSpec as P


def over_pieces(shard, axis):
    pieces = lax.all_gather(shard, axis).astype(jnp.float32)
    return pieces.sum(axis=0)


def from_everyone(shard, axis):
    count = lax.axis_size(axis)
    return lax.all_to_all(
        jnp.broadcast_to(shard[None], (count, *shard.shape)), axis, 0, 0, tiled=True
    )


def in_order(pieces, dim):
    pieces = jnp.moveaxis(pieces, 0, dim)
    dims = pieces.shape
    return pieces.reshape(*dims[:dim], dims[dim] * dims[dim + 1], *dims[dim + 2 :])


def gathered_copies(shard, axis, dim):
    pieces = from_everyone(shard, axis)
    return in_order(pieces, dim)


def taken_together(shard, axis):
    return from_everyone(shard, axis).astype(jnp.float32).sum(axis=0)


def cut_along(shard, dim, count):
    dims = shard.shape
    pieces = shard.reshape(*dims[:dim], count, dims[dim] // count, *dims[dim + 1 :])
    return jnp.moveaxis(pieces, dim, 0)


def sent_and_summed(shard, axis, dim):
    pieces = cut_along(shard, dim, lax.axis_size(axis))
    arrived = lax.all_to_all(pieces, axis, split_axis=0, concat_axis=0, tiled=True)
    return arrived.astype(jnp.float32).sum(axis=0)


def contract_first(left, right):
    return lax.dot_general(left, right, (((0,), (0,)), ((), ())), precision=lax.Precision.HIGHEST)


def shards(orbitals, kernel, block_vectors):
    groups = lax.axis_size("ga")
    own_band = lax.axis_index("band")
    total_coeffs = orbitals.shape[1] * groups
    full_orbitals, full_block = (
        lax.all_gather(orbitals, "band", axis=0, tiled=True),
        lax.all_gather(block_vectors, "band", axis=0, tiled=True),
    )
    weighted = (-(full_orbitals.astype(jnp.float32) * kernel[None, :])).astype(jnp.bfloat16)
    own_rows = orbitals.shape[0]
    partial_rows = lax.dot_general(
        orbitals, weighted, (((1,), (1,)), ((), ())), preferred_element_type=jnp.float32
    )
    summed_rows = over_pieces(partial_rows.astype(jnp.bfloat16), "ga").astype(jnp.float32)
    margin = (
        -gathered_copies(summed_rows.astype(jnp.bfloat16), "band", 0).astype(summed_rows.dtype)
        / total_coeffs
    )
    factor = jnp.linalg.cholesky(margin)
    identity = jnp.eye(factor.shape[0], dtype=jnp.float32)
    inverse = lax.linalg.triangular_solve(factor, identity, left_side=True, lower=True)
    inverse_rows = lax.dynamic_slice_in_dim(inverse, own_band * own_rows, own_rows, 0)
    projector = jnp.dot(inverse_rows, weighted.astype(jnp.float32), precision=lax.Precision.HIGHEST)
    local_coupling = jnp.dot(
        projector, full_block.astype(jnp.float32).T, precision=lax.Precision.HIGHEST
    )
    coupling = (
        taken_together(local_coupling.astype(jnp.bfloat16), "ga").astype(jnp.float32) / total_coeffs
    )
    applied = sent_and_summed(
        (-contract_first(coupling, projector)).astype(jnp.bfloat16), "band", 0
    )
    return (projector.astype(jnp.bfloat16), applied.astype(jnp.bfloat16))


def solution(mesh):
    placed = (P(("img", "band"), "ga"), P("ga"), P(("img", "band"), "ga"))
    return jax.shard_map(
        shards,
        mesh=mesh,
        in_specs=placed,
        out_specs=(P(("img", "band"), "ga"), P(("img", "band"), "ga")),
        check_vma=False,
    )
```

profile of v0, /device:TPU:513, one launch (start us, length us, event | category | flops | bytes accessed | tf_op | source)
XLA Modules:
  0.0 510.3 jit_solution(14080767505893318742)
XLA Ops:
  8.0 80.9 %all-gather.5.cloned.1.call-done = bf16[768,3072]{1,0:T(8,128)(2,1)} async-done(((bf16[96,3072]{1,0:T(8,128)(2,1)}), bf16[768,3072]{1,0:T(8,128)(2,1)}) %all-gather.5.cloned.1.call-update) | async-done | bytes 4718608 | tf_op jit(solution)/shard_map/all_gather | solution.py:55
  89.0 4.8 fusion.21
  93.8 41.2 %all-gather.9.cloned.1.call-done = bf16[1536,768]{1,0:T(8,128)(2,1)} async-done(((bf16[96,768]{1,0:T(8,128)(2,1)}), bf16[1536,768]{1,0:T(8,128)(2,1)}) %all-gather.9.cloned.1.call-update) | async-done | bytes 2359312 | tf_op jit(solution)/shard_map/all_gather | solution.py:8
  138.0 6.4 %all-to-all-start = ((bf16[8,96,768]{2,1,0:T(8,128)(2,1)}), bf16[8,96,768]{2,1,0:T(8,128)(2,1)S(1)}, u32[]{:S(2)}, u32[]{:S(2)}) async-start(bf16[8,96,768]{2,1,0:T(8,128)(2,1)} %broadcast_in_dim.5), calls=%async_computation | async-start | bytes 2359296 | tf_op jit(solution)/shard_map/all_to_all | solution.py:14
  147.9 35.2 %all-to-all-done = bf16[8,96,768]{2,1,0:T(8,128)(2,1)S(1)} async-done(((bf16[8,96,768]{2,1,0:T(8,128)(2,1)}), bf16[8,96,768]{2,1,0:T(8,128)(2,1)S(1)}, u32[]{:S(2)}, u32[]{:S(2)}) %all-to-all-start) | async-done | bytes 1179680 | tf_op jit(solution)/shard_map/all_to_all | solution.py:14
  188.9 11.7 %cholesky.165 = f32[128,128]{1,0:T(8,128)S(1)} custom-call(f32[128,128]{1,0:T(8,128)S(1)} %cholesky.424), custom_call_target="Cholesky" | custom-call | tf_op jit(solution)/shard_map/jit(cholesky)/cholesky | solution.py:68
  200.6 9.8 %custom-call.46 = f32[1,128,128]{1,2,0:T(8,128)S(1)} custom-call(f32[1,128,128]{2,1,0:T(8,128)S(1)} %get-tuple-element.45), custom_call_target="InvertDiagBlocksLowerTriangular" | custom-call | tf_op jit(solution)/shard_map/jit(cholesky)/cholesky | solution.py:68
  213.4 11.7 %cholesky.188 = f32[128,128]{1,0:T(8,128)S(1)} custom-call(f32[128,128]{1,0:T(8,128)S(1)} %cholesky.428), custom_call_target="Cholesky" | custom-call | tf_op jit(solution)/shard_map/jit(cholesky)/cholesky | solution.py:68
  225.2 10.0 %custom-call.47 = f32[1,128,128]{1,2,0:T(8,128)S(1)} custom-call(f32[1,128,128]{2,1,0:T(8,128)S(1)} %get-tuple-element.42), custom_call_target="InvertDiagBlocksLowerTriangular" | custom-call | tf_op jit(solution)/shard_map/jit(cholesky)/cholesky | solution.py:68
  237.1 11.7 %cholesky.354 = f32[128,128]{1,0:T(8,128)S(1)} custom-call(f32[128,128]{1,0:T(8,128)S(1)} %cholesky.433), custom_call_target="Cholesky" | custom-call | tf_op jit(solution)/shard_map/jit(cholesky)/cholesky | solution.py:68
  249.5 9.8 %custom-call.48 = f32[1,128,128]{1,2,0:T(8,128)S(1)} custom-call(f32[1,128,128]{2,1,0:T(8,128)S(1)} %get-tuple-element.39), custom_call_target="InvertDiagBlocksLowerTriangular" | custom-call | tf_op jit(solution)/shard_map/jit(cholesky)/cholesky | solution.py:68
  261.2 12.2 %cholesky.373 = f32[128,128]{1,0:T(8,128)S(1)} custom-call(f32[128,128]{1,0:T(8,128)S(1)} %cholesky.438), custom_call_target="Cholesky" | custom-call | tf_op jit(solution)/shard_map/jit(cholesky)/cholesky | solution.py:68
  274.1 9.8 %custom-call.49 = f32[1,128,128]{1,2,0:T(8,128)S(1)} custom-call(f32[1,128,128]{2,1,0:T(8,128)S(1)} %get-tuple-element.36), custom_call_target="InvertDiagBlocksLowerTriangular" | custom-call | tf_op jit(solution)/shard_map/jit(cholesky)/cholesky | solution.py:68
  285.7 11.7 %cholesky.392 = f32[128,128]{1,0:T(8,128)S(1)} custom-call(f32[128,128]{1,0:T(8,128)S(1)} %cholesky.443), custom_call_target="Cholesky" | custom-call | tf_op jit(solution)/shard_map/jit(cholesky)/cholesky | solution.py:68
  298.2 9.8 %custom-call.50 = f32[1,128,128]{1,2,0:T(8,128)S(1)} custom-call(f32[1,128,128]{2,1,0:T(8,128)S(1)} %get-tuple-element.33), custom_call_target="InvertDiagBlocksLowerTriangular" | custom-call | tf_op jit(solution)/shard_map/jit(cholesky)/cholesky | solution.py:68
  309.5 11.9 %cholesky.410 = f32[128,128]{1,0:T(8,128)S(1)} custom-call(f32[128,128]{1,0:T(8,128)S(1)} %convolution_subtract_fusion.8), custom_call_target="Cholesky" | custom-call | tf_op jit(solution)/shard_map/jit(cholesky)/cholesky | solution.py:68
  328.2 21.5 %while.1 = (s32[]{:T(128)}, f32[768,768]{1,0:T(8,128)}, s32[6,2]{0,1:T(2,128)S(1)}, f32[6,128,128]{2,1,0:T(8,128)}, s32[]{:T(128)}) while((s32[]{:T(128)}, f32[768,768]{1,0:T(8,128)}, s32[6,2]{0,1:T(2,128)S(1)}, f32[6,128,128]{2,1,0:T(8,128)}, s32[]{:T(128)}) %tuple.45), condition=%wide.while_cond, body=%wide.while_body.sunk | while | flops 2 | bytes 132705 | solution.py:70
  328.8 2.9 bitcast_dynamic-update-slice_fusion.2
  332.5 2.9 bitcast_dynamic-update-slice_fusion.2
  349.7 59.8 %custom-call.51 = f32[6,128,128]{1,2,0:T(8,128)S(1)} custom-call(f32[6,128,128]{2,1,0:T(8,128)} %get-tuple-element.9), custom_call_target="InvertDiagBlocksLowerTriangular" | custom-call | tf_op jit(solution)/shard_map/triangular_solve | solution.py:70
  422.6 3.7 fusion.65
  426.4 3.0 convolution_convert_fusion
  429.4 27.4 %all_to_all.15 = bf16[16,96,256]{2,1,0:T(8,128)(2,1)S(1)} all-to-all(bf16[16,96,256]{2,1,0:T(8,128)(2,1)S(1)} %broadcast_in_dim.7), channel_id=1, replica_groups=mesh['img'=2,'ga'=16,'band'=8] {'ga'}, dimensions={0} | all-to-all | bytes 1572864 | tf_op jit(solution)/shard_map/all_to_all | solution.py:14
  459.6 43.0 %all_to_all.16 = bf16[8,32,3072]{2,1,0:T(8,128)(2,1)S(1)} all-to-all(bf16[8,32,3072]{2,1,0:T(8,128)(2,1)S(1)} %bitcast.88), channel_id=1, replica_groups=mesh['img'=2,'ga'=16,'band'=8] {'band'}, dimensions={0} | all-to-all | bytes 3145728 | tf_op jit(solution)/shard_map/all_to_all | solution.py:42
  (87 shorter events, 60.9 us)
Async XLA Ops:
  7.2 81.8 %all-gather.5.cloned.1.call-start = ((), (), s32[]{:S(2)}) async-start(), calls=%async_computation.3 | async-start | bytes 5308416 | tf_op jit(solution)/shard_map/all_gather | solution.py:55
  8.0 127.0 %all-gather.9.cloned.1.call-start = ((), (), s32[]{:S(2)}) async-start(), calls=%async_computation.5 | async-start | bytes 2506752 | tf_op jit(solution)/shard_map/all_gather | solution.py:8
  138.0 45.0 %all-to-all-start = ((bf16[8,96,768]{2,1,0:T(8,128)(2,1)}), bf16[8,96,768]{2,1,0:T(8,128)(2,1)S(1)}, u32[]{:S(2)}, u32[]{:S(2)}) async-start(bf16[8,96,768]{2,1,0:T(8,128)(2,1)} %broadcast_in_dim.5), calls=%async_computation | async-start | bytes 2359296 | tf_op jit(solution)/shard_map/all_to_all | solution.py:14
  144.5 281.9 %all-gather.7.cloned.1.call-start = ((), (), s32[]{:S(2)}) async-start(), calls=%async_computation.4 | async-start | bytes 1769472 | tf_op jit(solution)/shard_map/all_gather | solution.py:56
  187.4 1.5 copy-start.1
  328.2 84.5 %copy-start = (f32[768,768]{1,0:T(8,128)S(1)}, f32[768,768]{1,0:T(8,128)}, u32[]{:S(2)}) copy-start(f32[768,768]{1,0:T(8,128)} %fusion.25) | copy-start | bytes 7077892
  414.7 7.9 %slice-start = ((s8[4718592]{0:T(1024)(128)(4,1)}), s8[4194304]{0:T(1024)(128)(4,1)S(1)}, s32[]{:S(2)}) async-start(s8[4718592]{0:T(1024)(128)(4,1)} %bitcast.90), calls=%async_computation.6 | async-start | bytes 8388608
  417.2 5.4 %slice-start.1 = ((s8[4718592]{0:T(1024)(128)(4,1)}), s8[524288]{0:T(1024)(128)(4,1)S(1)}, s32[]{:S(2)}) async-start(s8[4718592]{0:T(1024)(128)(4,1)} %bitcast.90), calls=%async_computation.7 | async-start | bytes 1048576
  419.2 3.4 copy-start.2
Sparse Core Ops, SparseCore 0:
  9.8 79.1 all-gather.4
  93.9 40.9 all-gather.8
  147.1 44.9 all-gather.6
where the time goes:
time: 514 us; the launch traced here: 510 us
  other arithmetic  193 us (38%)
  waiting for transfers between devices  159 us (31%)
  blocking collectives  70.4 us (14%)
  matrix products  37 us (7%)
  local copies, waits for them, and re-layouts  26.5 us (5%)
  between operations  18.2 us (4%)
  starting transfers between devices  6.6 us (1%)
    another operation x22, other arithmetic, shards(): factor = jnp.linalg.cholesky(margin)  124 us
    all_gather x1, waiting for transfers between devices, shards(): lax.all_gather(orbitals, 'band', axis=0, tiled=True)  80.9 us
    another operation x3, other arithmetic, shards(): lax.linalg.triangular_solve(factor, identity, left_side=True, lower=True)  61.4 us
    all_to_all x1, blocking collectives, sent_and_summed(): lax.all_to_all(pieces, axis, split_axis=0, concat_axis=0, tiled=True)  43 us
    all_gather x1, waiting for transfers between devices, over_pieces(): pieces = lax.all_gather(shard, axis).astype(jnp.float32)  41.2 us
    all_to_all x1, waiting for transfers between devices, from_everyone(): lax.all_to_all(jnp.broadcast_to(shard[None], (count, *shard.shape)), axis...  35.2 us
    all_to_all x1, blocking collectives, from_everyone(): lax.all_to_all(jnp.broadcast_to(shard[None], (count, *shard.shape)), axis...  27.4 us
    another operation x18, local copies, waits for them, and re-layouts  21.5 us
  transfers between devices with their start and end apart: 4, of which 3 were waited for; matrix products, arithmetic and copies ran while one was open for 47% of the time, Pallas kernels for 0%

commit v1 on v0

--- a/solution.py
+++ b/solution.py
@@ -2,6 +2,12 @@
 import jax.numpy as jnp
 from jax import lax
 from jax.sharding import PartitionSpec as P
+from jax.lax import all_to_all, axis_size
+
+
+def supply_weights_here(payload, axis_key="band"):
+    lower = jnp.concatenate(axis_size(axis_key) * [payload], axis=0)
+    return all_to_all(lower, axis_key, 0, 0, tiled=True)
 
 
 def over_pieces(shard, axis):
@@ -52,7 +58,7 @@
     own_band = lax.axis_index("band")
     total_coeffs = orbitals.shape[1] * groups
     full_orbitals, full_block = (
-        lax.all_gather(orbitals, "band", axis=0, tiled=True),
+        supply_weights_here(orbitals),
         lax.all_gather(block_vectors, "band", axis=0, tiled=True),
     )
     weighted = (-(full_orbitals.astype(jnp.float32) * kernel[None, :])).astype(jnp.bfloat16)

time: 514 us -> 568 us (1.11)
  blocking collectives: 70.4 us -> 170 us
  waiting for transfers between devices: 159 us -> 106 us
    all_to_all x0 -> x1, blocking collectives: none -> 99.4 us  [supply_weights_here(): return all_to_all(lower, axis_key, 0, 0, tiled=True)]
    all_gather x1 -> x0, waiting for transfers between devices: 80.9 us -> none  [shards(): lax.all_gather(orbitals, 'band', axis=0, tiled=True)]
    all_gather x1, waiting for transfers between devices: 41.2 us -> 70.3 us  [over_pieces(): pieces = lax.all_gather(shard, axis).astype(jnp.float32)]
  transfers between devices with their start and end apart: 4 -> 3, of which waited for: 3 -> 2; matrix products, arithmetic and copies ran while one was open for 47% -> 43% of each run, Pallas kernels for 0% -> 0%
where the time goes in v1:
time: 568 us; the launch traced here: 562 us
  other arithmetic  194 us (34%)
  blocking collectives  170 us (30%)
  waiting for transfers between devices  106 us (19%)
  matrix products  34 us (6%)
  local copies, waits for them, and re-layouts  31.2 us (5%)
  between operations  20.2 us (4%)
  starting transfers between devices  6.54 us (1%)
    another operation x22, other arithmetic, shards(): factor = jnp.linalg.cholesky(margin)  124 us
    all_to_all x1, blocking collectives, supply_weights_here(): return all_to_all(lower, axis_key, 0, 0, tiled=True)  99.4 us
    all_gather x1, waiting for transfers between devices, over_pieces(): pieces = lax.all_gather(shard, axis).astype(jnp.float32)  70.3 us
    another operation x3, other arithmetic, shards(): lax.linalg.triangular_solve(factor, identity, left_side=True, lower=True)  61.4 us
    all_to_all x1, blocking collectives, sent_and_summed(): lax.all_to_all(pieces, axis, split_axis=0, concat_axis=0, tiled=True)  42.9 us
    all_to_all x1, waiting for transfers between devices, from_everyone(): lax.all_to_all(jnp.broadcast_to(shard[None], (count, *shard.shape)), axis...  35.6 us
    all_to_all x1, blocking collectives, from_everyone(): lax.all_to_all(jnp.broadcast_to(shard[None], (count, *shard.shape)), axis...  27.4 us
    another operation x18, local copies, waits for them, and re-layouts  21.5 us
  transfers between devices with their start and end apart: 3, of which 2 were waited for; matrix products, arithmetic and copies ran while one was open for 43% of the time, Pallas kernels for 0%

profile of v1, /device:TPU:513, one launch (start us, length us, event | category | flops | bytes accessed | tf_op | source)
XLA Modules:
  0.0 562.4 jit_solution(13178203216048389176)
XLA Ops:
  10.7 99.4 %all_to_all.24 = bf16[8,96,3072]{2,1,0:T(8,128)(2,1)S(1)} all-to-all(bf16[8,96,3072]{2,1,0:T(8,128)(2,1)S(1)} %bitcast.97), channel_id=1, replica_groups=mesh['img'=2,'ga'=16,'band'=8] {'band'}, dimensions={0} | all-to-all | bytes 9437184 | tf_op jit(solution)/shard_map/all_to_all | solution.py:10
  116.1 70.3 %all-gather.6.cloned.1.call-done = bf16[1536,768]{1,0:T(8,128)(2,1)} async-done(((bf16[96,768]{1,0:T(8,128)(2,1)}), bf16[1536,768]{1,0:T(8,128)(2,1)}) %all-gather.6.cloned.1.call-update) | async-done | bytes 2359312 | tf_op jit(solution)/shard_map/all_gather | solution.py:14
  189.5 6.4 %all-to-all-start.1 = ((bf16[8,96,768]{2,1,0:T(8,128)(2,1)}), bf16[8,96,768]{2,1,0:T(8,128)(2,1)S(1)}, u32[]{:S(2)}, u32[]{:S(2)}) async-start(bf16[8,96,768]{2,1,0:T(8,128)(2,1)} %broadcast_in_dim.5), calls=%async_computation.1 | async-start | bytes 2359296 | tf_op jit(solution)/shard_map/all_to_all | solution.py:20
  199.1 35.6 %all-to-all-done.1 = bf16[8,96,768]{2,1,0:T(8,128)(2,1)S(1)} async-done(((bf16[8,96,768]{2,1,0:T(8,128)(2,1)}), bf16[8,96,768]{2,1,0:T(8,128)(2,1)S(1)}, u32[]{:S(2)}, u32[]{:S(2)}) %all-to-all-start.1) | async-done | bytes 1179680 | tf_op jit(solution)/shard_map/all_to_all | solution.py:20
  240.6 11.7 %cholesky.165 = f32[128,128]{1,0:T(8,128)S(1)} custom-call(f32[128,128]{1,0:T(8,128)S(1)} %cholesky.424), custom_call_target="Cholesky" | custom-call | tf_op jit(solution)/shard_map/jit(cholesky)/cholesky | solution.py:74
  252.3 9.8 %custom-call.46 = f32[1,128,128]{1,2,0:T(8,128)S(1)} custom-call(f32[1,128,128]{2,1,0:T(8,128)S(1)} %get-tuple-element.45), custom_call_target="InvertDiagBlocksLowerTriangular" | custom-call | tf_op jit(solution)/shard_map/jit(cholesky)/cholesky | solution.py:74
  265.1 11.7 %cholesky.188 = f32[128,128]{1,0:T(8,128)S(1)} custom-call(f32[128,128]{1,0:T(8,128)S(1)} %cholesky.428), custom_call_target="Cholesky" | custom-call | tf_op jit(solution)/shard_map/jit(cholesky)/cholesky | solution.py:74
  276.8 10.2 %custom-call.47 = f32[1,128,128]{1,2,0:T(8,128)S(1)} custom-call(f32[1,128,128]{2,1,0:T(8,128)S(1)} %get-tuple-element.42), custom_call_target="InvertDiagBlocksLowerTriangular" | custom-call | tf_op jit(solution)/shard_map/jit(cholesky)/cholesky | solution.py:74
  289.0 11.7 %cholesky.354 = f32[128,128]{1,0:T(8,128)S(1)} custom-call(f32[128,128]{1,0:T(8,128)S(1)} %cholesky.433), custom_call_target="Cholesky" | custom-call | tf_op jit(solution)/shard_map/jit(cholesky)/cholesky | solution.py:74
  301.4 9.8 %custom-call.48 = f32[1,128,128]{1,2,0:T(8,128)S(1)} custom-call(f32[1,128,128]{2,1,0:T(8,128)S(1)} %get-tuple-element.39), custom_call_target="InvertDiagBlocksLowerTriangular" | custom-call | tf_op jit(solution)/shard_map/jit(cholesky)/cholesky | solution.py:74
  313.1 11.9 %cholesky.373 = f32[128,128]{1,0:T(8,128)S(1)} custom-call(f32[128,128]{1,0:T(8,128)S(1)} %cholesky.438), custom_call_target="Cholesky" | custom-call | tf_op jit(solution)/shard_map/jit(cholesky)/cholesky | solution.py:74
  325.7 9.8 %custom-call.49 = f32[1,128,128]{1,2,0:T(8,128)S(1)} custom-call(f32[1,128,128]{2,1,0:T(8,128)S(1)} %get-tuple-element.36), custom_call_target="InvertDiagBlocksLowerTriangular" | custom-call | tf_op jit(solution)/shard_map/jit(cholesky)/cholesky | solution.py:74
  337.3 11.7 %cholesky.392 = f32[128,128]{1,0:T(8,128)S(1)} custom-call(f32[128,128]{1,0:T(8,128)S(1)} %cholesky.443), custom_call_target="Cholesky" | custom-call | tf_op jit(solution)/shard_map/jit(cholesky)/cholesky | solution.py:74
  349.7 9.8 %custom-call.50 = f32[1,128,128]{1,2,0:T(8,128)S(1)} custom-call(f32[1,128,128]{2,1,0:T(8,128)S(1)} %get-tuple-element.33), custom_call_target="InvertDiagBlocksLowerTriangular" | custom-call | tf_op jit(solution)/shard_map/jit(cholesky)/cholesky | solution.py:74
  361.1 11.9 %cholesky.410 = f32[128,128]{1,0:T(8,128)S(1)} custom-call(f32[128,128]{1,0:T(8,128)S(1)} %convolution_subtract_fusion.8), custom_call_target="Cholesky" | custom-call | tf_op jit(solution)/shard_map/jit(cholesky)/cholesky | solution.py:74
  379.8 21.5 %while.1 = (s32[]{:T(128)}, f32[768,768]{1,0:T(8,128)}, s32[6,2]{0,1:T(2,128)S(1)}, f32[6,128,128]{2,1,0:T(8,128)}, s32[]{:T(128)}) while((s32[]{:T(128)}, f32[768,768]{1,0:T(8,128)}, s32[6,2]{0,1:T(2,128)S(1)}, f32[6,128,128]{2,1,0:T(8,128)}, s32[]{:T(128)}) %tuple.45), condition=%wide.while_cond, body=%wide.while_body.sunk | while | flops 2 | bytes 132705 | solution.py:76
  380.5 2.9 bitcast_dynamic-update-slice_fusion.2
  384.1 2.9 bitcast_dynamic-update-slice_fusion.2
  387.7 2.9 bitcast_dynamic-update-slice_fusion.2
  401.3 59.8 %custom-call.51 = f32[6,128,128]{1,2,0:T(8,128)S(1)} custom-call(f32[6,128,128]{2,1,0:T(8,128)} %get-tuple-element.9), custom_call_target="InvertDiagBlocksLowerTriangular" | custom-call | tf_op jit(solution)/shard_map/triangular_solve | solution.py:76
  474.2 3.2 fusion.65
  477.5 3.0 convolution_convert_fusion.1
  480.5 27.4 %all_to_all.25 = bf16[16,96,256]{2,1,0:T(8,128)(2,1)S(1)} all-to-all(bf16[16,96,256]{2,1,0:T(8,128)(2,1)S(1)} %broadcast_in_dim.7), channel_id=1, replica_groups=mesh['img'=2,'ga'=16,'band'=8] {'ga'}, dimensions={0} | all-to-all | bytes 1572864 | tf_op jit(solution)/shard_map/all_to_all | solution.py:20
  510.7 42.9 %all_to_all.26 = bf16[8,32,3072]{2,1,0:T(8,128)(2,1)S(1)} all-to-all(bf16[8,32,3072]{2,1,0:T(8,128)(2,1)S(1)} %bitcast.96), channel_id=1, replica_groups=mesh['img'=2,'ga'=16,'band'=8] {'band'}, dimensions={0} | all-to-all | bytes 3145728 | tf_op jit(solution)/shard_map/all_to_all | solution.py:48
  (98 shorter events, 65.5 us)
Async XLA Ops:
  8.0 2.3 copy-start
  8.0 178.3 %all-gather.6.cloned.1.call-start = ((), (), s32[]{:S(2)}) async-start(), calls=%async_computation.5 | async-start | bytes 2506752 | tf_op jit(solution)/shard_map/all_gather | solution.py:14
  10.7 99.4 %copy-start.4 = (f32[3072]{0:T(1024)S(1)}, f32[3072]{0:T(1024)}, u32[]{:S(2)}) copy-start(f32[3072]{0:T(1024)} %param.4) | copy-start | bytes 36868
  111.6 2.1 copy-start.1
  189.5 45.2 %all-to-all-start.1 = ((bf16[8,96,768]{2,1,0:T(8,128)(2,1)}), bf16[8,96,768]{2,1,0:T(8,128)(2,1)S(1)}, u32[]{:S(2)}, u32[]{:S(2)}) async-start(bf16[8,96,768]{2,1,0:T(8,128)(2,1)} %broadcast_in_dim.5), calls=%async_computation.1 | async-start | bytes 2359296 | tf_op jit(solution)/shard_map/all_to_all | solution.py:20
  195.9 281.6 %all-gather.4.cloned.1.call-start = ((), (), s32[]{:S(2)}) async-start(), calls=%async_computation.4 | async-start | bytes 1769472 | tf_op jit(solution)/shard_map/all_gather | solution.py:62
  239.1 1.5 copy-start.3
  379.8 84.5 %copy-start.2 = (f32[768,768]{1,0:T(8,128)S(1)}, f32[768,768]{1,0:T(8,128)}, u32[]{:S(2)}) copy-start(f32[768,768]{1,0:T(8,128)} %fusion.24) | copy-start | bytes 7077892
  466.3 7.9 %slice-start = ((s8[4718592]{0:T(1024)(128)(4,1)}), s8[4194304]{0:T(1024)(128)(4,1)S(1)}, s32[]{:S(2)}) async-start(s8[4718592]{0:T(1024)(128)(4,1)} %bitcast.93), calls=%async_computation.6 | async-start | bytes 8388608
  468.8 5.4 slice-start.1
Sparse Core Ops, SparseCore 0:
  116.2 70.1 all-gather.5
Sparse Core Ops, SparseCore 1:
  198.2 45.3 all-gather.3
